TPU v7x, 32 devices: a whole 2x2x4 slice. The times are simulated.
32 devices in a mesh: dp: 8 (over z, x), rep: 4 (over y, core).
Axes of the slice: x: 2, y: 2, z: 4, core: 2. Of those that a mesh axis runs over, the one named last changes fastest.
Arguments:
- token_inputs: bfloat16 [16384, 2048], P(('dp', 'rep')), may hold values from -12 to 12
- cotangent: bfloat16 [16384, 2048], P(('dp', 'rep')), may hold values from -6 to 6
- gate_preact: bfloat16 [16384, 768], P(('dp', 'rep')), may hold values from -6 to 6
- up_preact: bfloat16 [16384, 768], P(('dp', 'rep')), may hold values from -6 to 6
- down_weight: bfloat16 [2, 768, 2048], P(None, None, 'dp'), may hold values from -0.21875 to 0.21875
- block_expert: int32 [128], P(('dp', 'rep')), may hold values from 0 to 1
- block_count: int32 [128], P(('dp', 'rep')), may hold values from 1 to 128, as said below
Outputs:
- update: bfloat16 [2, 3, 768, 2048], P(None, None, None, 'dp')
Inputs may be any that keep to these rules, and one draw needn't show every extreme that they name: `block_count`: live rows of a block, at most 128; in every draw some block is full.
All inputs are finite; a program needn't handle non-finite values.
Results may differ from a plain program's by a relative error of at most 0.02.
Values may be sent and summed in bfloat16 or wider, within the bound.
A program may use at most 128 MiB of HBM per device.

v0:
```python
import math
import jax
import jax.numpy as jnp
from jax import lax
from jax.sharding import PartitionSpec as P

D = 2048
ITERS = 2
ns_first = 3.4445
ns_second = -4.775
ns_third = 2.0315
norm_eps = 1e-07


def whole_sweeps(matrix, column_width, groups_all, sweeps, scale):
    hidden_width = matrix.shape[0]
    group = math.gcd(8, groups_all)
    current = matrix
    result = None
    for sweep in range(sweeps):

        def add_group(index, total):
            cols = lax.dynamic_slice_in_dim(
                current, index * group * column_width, group * column_width, 1
            )
            cols = cols.reshape(hidden_width, group, column_width)
            term = jnp.einsum(
                "fnd,gnd->nfg", cols, cols, preferred_element_type=jnp.float32
            ).astype(jnp.bfloat16)
            return total + jnp.sum(lax.optimization_barrier(term).astype(jnp.float32), axis=0)

        gram = lax.fori_loop(
            0, groups_all // group, add_group, jnp.zeros((hidden_width, hidden_width), jnp.float32)
        )
        gram_half = gram.astype(jnp.bfloat16)
        squared = jnp.dot(gram_half, gram_half, preferred_element_type=jnp.float32)
        poly = (ns_second * gram + ns_third * squared).astype(jnp.bfloat16)
        newer = ns_first * current.astype(jnp.float32) + jnp.dot(
            poly, current, preferred_element_type=jnp.float32
        )
        if sweep + 1 < sweeps:
            current = newer.astype(jnp.bfloat16)
        else:
            result = (scale * newer).astype(jnp.bfloat16)
    return result


def per_device(
    token_inputs, cotangent, gate_preact, up_preact, down_weight, block_expert, block_count
):
    blocks = block_count.shape[0]
    rows_here = token_inputs.shape[0]
    hidden_width = gate_preact.shape[1]
    width = token_inputs.shape[1]
    block_rows = rows_here // blocks
    experts_here = down_weight.shape[0]
    row_place = jnp.arange(rows_here, dtype=jnp.int32) % block_rows
    row_count = jnp.repeat(block_count, block_rows, total_repeat_length=rows_here)
    row_expert = jnp.repeat(block_expert, block_rows, total_repeat_length=rows_here)
    live_rows = row_place < row_count
    masked = jnp.where(live_rows[:, None], cotangent, jnp.zeros_like(cotangent))
    gate = gate_preact.astype(jnp.float32)
    upper = up_preact.astype(jnp.float32)
    sigmoid_gate = jax.nn.sigmoid(gate)
    hidden = (gate * sigmoid_gate * upper).astype(jnp.bfloat16)
    selector = (row_expert[None, :] == jnp.arange(experts_here, dtype=jnp.int32)[:, None]).astype(
        jnp.bfloat16
    )
    masked_each = masked[None, :, :] * selector[:, :, None]
    weights_all = lax.all_gather(down_weight, "dp", axis=2, tiled=True)
    back = jnp.einsum("erd,efd->rf", masked_each, weights_all, preferred_element_type=jnp.float32)
    grad_gate = (back * upper * sigmoid_gate * (1.0 + gate * (1.0 - sigmoid_gate))).astype(
        jnp.bfloat16
    )
    grad_up = (back * gate * sigmoid_gate).astype(jnp.bfloat16)
    gate_up = jnp.concatenate([grad_gate, grad_up], axis=1)
    gate_up_each = gate_up[None, :, :] * selector[:, :, None]
    hidden_each = hidden[None, :, :] * selector[:, :, None]
    input_part = jnp.einsum(
        "erf,rd->efd", gate_up_each, token_inputs, preferred_element_type=jnp.float32
    )
    output_part = jnp.einsum("erf,rd->efd", hidden_each, masked, preferred_element_type=jnp.float32)
    partial_value = jnp.concatenate(
        [input_part.reshape(experts_here, 2, hidden_width, width), output_part[:, None]], axis=1
    )
    partial_half = partial_value.astype(jnp.bfloat16)
    terms = lax.optimization_barrier(partial_half).astype(jnp.float32)
    grad = lax.psum_scatter(
        terms.astype(jnp.bfloat16), "dp", scatter_dimension=3, tiled=True
    ).astype(jnp.float32)
    grad = lax.psum(grad.astype(jnp.bfloat16), "rep").astype(jnp.float32)
    squares = lax.psum(jnp.sum(grad * grad, axis=(2, 3)), "dp")
    current = (grad / (jnp.sqrt(squares) + norm_eps)[:, :, None, None]).astype(jnp.bfloat16)
    column_width = current.shape[3]
    scale = jnp.sqrt(jnp.float32(D))
    result = None
    n_dp = lax.axis_size("dp")
    matrices = experts_here * 3
    flat = current.reshape(matrices, hidden_width, column_width)
    padding = jnp.zeros((n_dp - matrices, hidden_width, column_width), jnp.bfloat16)
    outbound = jnp.concatenate([flat, padding], axis=0)
    owned = lax.all_to_all(outbound, "dp", split_axis=0, concat_axis=2, tiled=True)
    finished = whole_sweeps(owned[0], column_width, n_dp, ITERS, scale)
    returned = lax.all_to_all(finished[None], "dp", split_axis=2, concat_axis=0, tiled=True)
    result = returned[:matrices].reshape(experts_here, 3, hidden_width, column_width)
    return result


def solution(mesh):
    placed = (
        P(("dp", "rep"), None),
        P(("dp", "rep"), None),
        P(("dp", "rep"), None),
        P(("dp", "rep"), None),
        P(None, None, "dp"),
        P(("dp", "rep")),
        P(("dp", "rep")),
    )
    return jax.shard_map(
        per_device, mesh=mesh, in_specs=placed, out_specs=P(None, None, None, "dp"), check_vma=False
    )
```

profile of v0, /device:TPU:0, one launch (start us, length us, event | category | flops | bytes accessed | tf_op | source)
XLA Modules:
  0.0 795.3 jit_solution(15564926438498596758)
XLA Ops:
  6.5 0.0 copy-start
  6.5 0.0 all-gather.2.cloned.1.call-start
  6.5 0.7 all-gather.2.cloned.1.call-update
  7.3 0.0 reduce-scatter.2.cloned.1.call-start
  7.3 1.4 fusion.46
  8.7 2.5 fusion.34
  11.2 1.4 fusion.45
  12.6 2.5 select_select_fusion
  15.2 3.1 broadcast_select_fusion
  18.3 93.3 %all-gather.2.cloned.1.call-done = bf16[2,768,2048]{2,1,0:T(8,128)(2,1)} async-done(((bf16[2,768,256]{2,1,0:T(8,128)(2,1)}), bf16[2,768,2048]{2,1,0:T(8,128)(2,1)}) %all-gather.2.cloned.1.call-update) | async-done | bytes 6291472 | tf_op jit(solution)/shard_map/all_gather | solution.py:70
  111.6 7.8 fusion.15
  119.4 1.3 pad_maximum_fusion.1
  120.7 2.6 copy.31
  123.3 1.2 copy.32
  124.5 5.5 convert_bitcast_fusion
  129.9 0.0 copy-done
  130.0 0.0 copy-done.3
  130.0 6.9 convolution_convert_fusion
  136.9 10.4 %pad_maximum_fusion = bf16[2,3,768,2048]{3,2,1,0:T(8,128)(2,1)} fusion(bf16[2,1,768,2048]{3,2,1,0:T(8,128)(2,1)S(1)} %convert_bitcast_fusion, bf16[2,2,768,2048]{3,2,1,0:T(8,128)(2,1)S(1)} %bitcast.77), kind=kLoop, calls=%fused_computation | loop fusion | flops 9437184 | bytes 37748736 | tf_op jit(solution)/shard_map/concatenate | solution.py:83
  147.3 0.0 reduce-scatter.2.cloned.1.call-update
  147.4 0.0 all-reduce.3.cloned.1.call-start
  147.4 308.6 %reduce-scatter.2.cloned.1.call-done = bf16[2,3,768,256]{3,2,1,0:T(8,128)(2,1)} async-done(((bf16[2,3,768,2048]{3,2,1,0:T(8,128)(2,1)}), bf16[2,3,768,256]{3,2,1,0:T(8,128)(2,1)}) %reduce-scatter.2.cloned.1.call-update) | async-done | bytes 2359312 | tf_op jit(solution)/shard_map/reduce_scatter | solution.py:88
  456.1 0.0 all-reduce.3.cloned.1.call-update
  456.1 57.2 %all-reduce.3.cloned.1.call-done = bf16[2,3,768,256]{3,2,1,0:T(8,128)(2,1)} async-done(((bf16[2,3,768,256]{3,2,1,0:T(8,128)(2,1)}), bf16[2,3,768,256]{3,2,1,0:T(8,128)(2,1)}) %all-reduce.3.cloned.1.call-update) | async-done | bytes 2359312 | tf_op jit(solution)/shard_map/psum | solution.py:91
  513.2 2.5 fusion
  515.7 21.3 %psum.15 = f32[2,3]{1,0:T(2,128)S(1)} all-reduce(f32[2,3]{1,0:T(2,128)S(1)} %fusion), channel_id=1, replica_groups=mesh['dp'=8,'rep'=4] {'dp'}, use_global_device_ids=true, to_apply=%region_3.5 | all-reduce | flops 6 | bytes 48 | tf_op jit(solution)/shard_map/psum | solution.py:92
  537.0 0.0 copy-done.2
  537.0 0.9 fusion.1
  538.0 0.2 concatenate.18
  538.2 70.2 %all_to_all.30 = bf16[8,768,256]{2,1,0:T(8,128)(2,1)} all-to-all(bf16[8,768,256]{2,1,0:T(8,128)(2,1)S(1)} %concatenate.18), channel_id=1, replica_groups=mesh['dp'=8,'rep'=4] {'dp'}, dimensions={0} | all-to-all | bytes 6291456 | tf_op jit(solution)/shard_map/all_to_all | solution.py:102
  608.4 5.5 convolution_convert_fusion.2
  613.9 2.7 convert_reduce_fusion.1
  616.6 3.2 copy.34
  619.8 3.0 copy.35
  622.8 9.3 %add_convert_fusion = bf16[768,2048]{1,0:T(8,128)(2,1)} fusion(bf16[768,2048]{1,0:T(8,128)(2,1)} %copy.35, bf16[768,2048]{0,1:T(8,128)(2,1)S(1)} %bitcast.76, f32[768,768]{1,0:T(8,128)} %convert_reduce_fusion.1), kind=kOutput, calls=%fused_computation.7 | convolution fusion | flops 3331129344 | bytes 11796480 | tf_op jit(solution)/shard_map/dot_general | solution.py:38
  632.1 5.5 convolution_convert_fusion.1
  637.6 2.7 convert_reduce_fusion
  640.4 8.7 %fusion.8 = bf16[1,768,2048]{2,1,0:T(8,128)(2,1)S(1)} fusion(bf16[768,2048]{1,0:T(8,128)(2,1)} %add_convert_fusion, f32[768,768]{1,0:T(8,128)} %convert_reduce_fusion), kind=kOutput, calls=%fused_computation.19 | convolution fusion | flops 3332702208 | bytes 8650752 | tf_op jit(solution)/shard_map/dot_general | solution.py:38
  649.1 11.2 %copy.38 = bf16[1,768,2048]{1,0,2:T(2,128)(2,1)} copy(bf16[1,768,2048]{2,1,0:T(8,128)(2,1)S(1)} %fusion.8) | data formatting | bytes 6291456 | tf_op jit(solution)/shard_map/broadcast_in_dim | solution.py:104
  660.3 0.5 broadcast.198
  660.8 33.5 %reduce.3 = bf16[2048,768]{1,0:T(8,128)(2,1)} reduce(bf16[2048,1,768]{2,1,0:T(2,128)(2,1)} %bitcast.73, bf16[]{:T(256)} %broadcast.198), dimensions={1}, to_apply=%bitcast.67.reduce_sub_computation | reduce | bytes 6291458
  694.3 4.6 reshape.141
  699.0 72.8 %all_to_all.31 = bf16[8,2,98304]{2,1,0:T(2,128)(2,1)} all-to-all(bf16[8,2,98304]{2,1,0:T(2,128)(2,1)S(1)} %reshape.141), channel_id=1, replica_groups=mesh['dp'=8,'rep'=4] {'dp'}, dimensions={0} | all-to-all | bytes 6291456 | tf_op jit(solution)/shard_map/all_to_all | solution.py:104
  771.8 7.8 reshape.142
  779.6 3.3 copy.40
  782.9 0.0 copy-start.1
  782.9 1.6 slice.46
  784.5 4.3 copy.39
  (5 shorter events, 0.0 us)
Async XLA Ops:
  6.5 123.4 %copy-start = (bf16[512,2048]{1,0:T(8,128)(2,1)S(1)}, bf16[512,2048]{1,0:T(8,128)(2,1)}, u32[]{:S(2)}) copy-start(bf16[512,2048]{1,0:T(8,128)(2,1)} %param.13) | copy-start | bytes 6291460
  6.5 105.1 %all-gather.2.cloned.1.call-start = ((), (), s32[]{:S(2)}) async-start(), calls=%async_computation.3 | async-start | bytes 7077888 | tf_op jit(solution)/shard_map/all_gather | solution.py:70
  7.3 448.8 %reduce-scatter.2.cloned.1.call-start = ((), (), s32[]{:S(2)}) async-start(), calls=%async_computation.4 | async-start | bytes 21233664 | tf_op jit(solution)/shard_map/reduce_scatter | solution.py:88
  124.5 5.5 copy-start.3
  147.4 365.9 %all-reduce.3.cloned.1.call-start = ((), (), s32[]{:S(2)}) async-start(), calls=%async_computation.5 | async-start | bytes 4718592 | tf_op jit(solution)/shard_map/psum | solution.py:91
  513.2 23.8 %copy-start.2 = (bf16[2,3,768,256]{3,2,1,0:T(8,128)(2,1)S(1)}, bf16[2,3,768,256]{3,2,1,0:T(8,128)(2,1)}, u32[]{:S(2)}) copy-start(bf16[2,3,768,256]{3,2,1,0:T(8,128)(2,1)} %all-reduce.3.cloned.1.call-done) | copy-start | bytes 7077892
  782.9 5.9 copy-start.1
Sparse Core Ops, SparseCore 0:
  9.4 102.1 all-gather.1
  147.5 308.5 reduce-scatter.1
  458.4 54.7 all-reduce.2
where the time goes:
time: 796 us; the launch traced here: 795 us
  waiting for transfers between devices  460 us (58%)
  blocking collectives  164 us (21%)
  other arithmetic  62.2 us (8%)
  matrix products  49.3 us (6%)
  local copies, waits for them, and re-layouts  46.3 us (6%)
  between operations  13.2 us (2%)
    reduce_scatter x1, waiting for transfers between devices, per_device(): lax.psum_scatter(terms.astype(jnp.bfloat16), 'dp', scatter_dimension=3, t...  309 us
    all_gather x1, waiting for transfers between devices, per_device(): weights_all = lax.all_gather(down_weight, 'dp', axis=2, tiled=True)  93.3 us
    all_to_all x1, blocking collectives, per_device(): lax.all_to_all(finished[None], 'dp', split_axis=2, concat_axis=0, tiled=T...  72.8 us
    all_to_all x1, blocking collectives, per_device(): lax.all_to_all(outbound, 'dp', split_axis=0, concat_axis=2, tiled=True)  70.2 us
    psum x1, waiting for transfers between devices, per_device(): grad = lax.psum(grad.astype(jnp.bfloat16), 'rep').astype(jnp.float32)  57.2 us
    unnamed x1, other arithmetic  33.5 us
    psum x1, blocking collectives, per_device(): squares = lax.psum(jnp.sum(grad * grad, axis=(2, 3)), 'dp')  21.3 us
    dot_general x2, matrix products, whole_sweeps(): jnp.dot(poly, current, preferred_element_type=jnp.float32)  18 us
  transfers between devices with their start and end apart: 3, of which 3 were waited for; matrix products, arithmetic and copies ran while one was open for 1% of the time, Pallas kernels for 0%

commit v1 on v0

--- a/solution.py
+++ b/solution.py
@@ -101,7 +101,11 @@
     outbound = jnp.concatenate([flat, padding], axis=0)
     owned = lax.all_to_all(outbound, "dp", split_axis=0, concat_axis=2, tiled=True)
     finished = whole_sweeps(owned[0], column_width, n_dp, ITERS, scale)
-    returned = lax.all_to_all(finished[None], "dp", split_axis=2, concat_axis=0, tiled=True)
+    block = finished[None]
+    size = lax.axis_size("dp")
+    parts = jnp.stack(jnp.split(block, size, axis=2), axis=0)
+    parts = lax.all_to_all(parts, "dp", split_axis=0, concat_axis=0)
+    returned = jnp.concatenate(parts, axis=0)
     result = returned[:matrices].reshape(experts_here, 3, hidden_width, column_width)
     return result
 

time: 796 us -> 733 us (0.921)
  other arithmetic: 62.2 us -> 28.6 us
  local copies, waits for them, and re-layouts: 46.3 us -> 16.8 us
    unnamed x1 -> x0, other arithmetic: 33.5 us -> none
    unnamed x12 -> x17, local copies, waits for them, and re-layouts: 16.2 us -> 0.39 us
    broadcast_in_dim x1 -> x0, local copies, waits for them, and re-layouts: 11.2 us -> none  [per_device(): finished[None]]
where the time goes in v1:
time: 733 us
  waiting for transfers between devices  460 us (63%)
  blocking collectives  164 us (22%)
  matrix products  50.3 us (7%)
  other arithmetic  28.6 us (4%)
  local copies, waits for them, and re-layouts  16.8 us (2%)
  between operations  13.3 us (2%)
    reduce_scatter x1, waiting for transfers between devices, per_device(): lax.psum_scatter(terms.astype(jnp.bfloat16), 'dp', scatter_dimension=3, t...  309 us
    all_gather x1, waiting for transfers between devices, per_device(): weights_all = lax.all_gather(down_weight, 'dp', axis=2, tiled=True)  93.3 us
    all_to_all x1, blocking collectives, per_device(): parts = lax.all_to_all(parts, 'dp', split_axis=0, concat_axis=0)  72.9 us
    all_to_all x1, blocking collectives, per_device(): lax.all_to_all(outbound, 'dp', split_axis=0, concat_axis=2, tiled=True)  69.4 us
    psum x1, waiting for transfers between devices, per_device(): grad = lax.psum(grad.astype(jnp.bfloat16), 'rep').astype(jnp.float32)  57.2 us
    psum x1, blocking collectives, per_device(): squares = lax.psum(jnp.sum(grad * grad, axis=(2, 3)), 'dp')  21.3 us
    dot_general x2, matrix products, whole_sweeps(): jnp.dot(poly, current, preferred_element_type=jnp.float32)  19 us
  transfers between devices with their start and end apart: 3, of which 3 were waited for; matrix products, arithmetic and copies ran while one was open for 1% of the time, Pallas kernels for 0%

profile of v1, /device:TPU:0, one launch (start us, length us, event | category | flops | bytes accessed | tf_op | source)
XLA Modules:
  0.0 732.6 jit_solution(7592095148430692616)
XLA Ops:
  6.5 0.0 copy-start
  6.5 0.0 all-gather.2.cloned.1.call-start
  6.5 0.7 all-gather.2.cloned.1.call-update
  7.3 0.0 reduce-scatter.2.cloned.1.call-start
  7.3 1.4 fusion.54
  8.7 2.5 fusion.42
  11.2 1.4 fusion.53
  12.6 2.5 select_select_fusion
  15.2 3.1 broadcast_select_fusion
  18.3 93.3 %all-gather.2.cloned.1.call-done = bf16[2,768,2048]{2,1,0:T(8,128)(2,1)} async-done(((bf16[2,768,256]{2,1,0:T(8,128)(2,1)}), bf16[2,768,2048]{2,1,0:T(8,128)(2,1)}) %all-gather.2.cloned.1.call-update) | async-done | bytes 6291472 | tf_op jit(solution)/shard_map/all_gather | solution.py:70
  111.6 7.8 %fusion.15 = (bf16[512,768]{1,0:T(8,128)(2,1)S(1)}, bf16[512,768]{1,0:T(8,128)(2,1)S(1)}, bf16[512,768]{1,0:T(8,128)(2,1)S(1)}) fusion(bf16[512,768]{1,0:T(8,128)(2,1)} %param.16, bf16[512,768]{1,0:T(8,128)(2,1)} %param.15, bf16[2,768,2048]{2,1,0:T(8,128)(2,1)} %all-gather.2.cloned.1.call-done, bf16[2,512]{1,0:T(2,128)(2,1)S(1)} %compare_convert_fusion, ...), kind=kOutput, calls=%fused_computation.35 | convolution fusion | flops 3230400512 | bytes 12322816 | tf_op jit(solution)/shard_map/erd,efd->rf/dot_general | solution.py:71
  119.4 1.3 pad_maximum_fusion.1
  120.7 2.6 copy.13
  123.3 1.2 copy.14
  124.5 5.5 convert_bitcast_fusion
  129.9 0.0 copy-done
  130.0 0.0 copy-done.4
  130.0 6.9 convolution_convert_fusion
  136.9 10.4 %pad_maximum_fusion = bf16[2,3,768,2048]{3,2,1,0:T(8,128)(2,1)} fusion(bf16[2,1,768,2048]{3,2,1,0:T(8,128)(2,1)S(1)} %convert_bitcast_fusion, bf16[2,2,768,2048]{3,2,1,0:T(8,128)(2,1)S(1)} %bitcast.102), kind=kLoop, calls=%fused_computation | loop fusion | flops 9437184 | bytes 37748736 | tf_op jit(solution)/shard_map/concatenate | solution.py:83
  147.3 0.0 reduce-scatter.2.cloned.1.call-update
  147.4 0.0 all-reduce.3.cloned.1.call-start
  147.4 308.6 %reduce-scatter.2.cloned.1.call-done = bf16[2,3,768,256]{3,2,1,0:T(8,128)(2,1)} async-done(((bf16[2,3,768,2048]{3,2,1,0:T(8,128)(2,1)}), bf16[2,3,768,256]{3,2,1,0:T(8,128)(2,1)}) %reduce-scatter.2.cloned.1.call-update) | async-done | bytes 2359312 | tf_op jit(solution)/shard_map/reduce_scatter | solution.py:88
  456.1 0.0 all-reduce.3.cloned.1.call-update
  456.1 57.2 %all-reduce.3.cloned.1.call-done = bf16[2,3,768,256]{3,2,1,0:T(8,128)(2,1)} async-done(((bf16[2,3,768,256]{3,2,1,0:T(8,128)(2,1)}), bf16[2,3,768,256]{3,2,1,0:T(8,128)(2,1)}) %all-reduce.3.cloned.1.call-update) | async-done | bytes 2359312 | tf_op jit(solution)/shard_map/psum | solution.py:91
  513.2 2.5 fusion
  515.7 21.3 %psum.15 = f32[2,3]{1,0:T(2,128)S(1)} all-reduce(f32[2,3]{1,0:T(2,128)S(1)} %fusion), channel_id=1, replica_groups=mesh['dp'=8,'rep'=4] {'dp'}, use_global_device_ids=true, to_apply=%region_3.5 | all-reduce | flops 6 | bytes 48 | tf_op jit(solution)/shard_map/psum | solution.py:92
  537.0 0.9 fusion.1
  538.0 0.2 concatenate.18
  538.2 69.4 %all_to_all.20 = bf16[8,768,256]{2,1,0:T(8,128)(2,1)S(1)} all-to-all(bf16[8,768,256]{2,1,0:T(8,128)(2,1)S(1)} %concatenate.18), channel_id=1, replica_groups=mesh['dp'=8,'rep'=4] {'dp'}, dimensions={0} | all-to-all | bytes 6291456 | tf_op jit(solution)/shard_map/all_to_all | solution.py:102
  607.7 3.2 copy.16
  610.9 4.8 copy.17
  615.6 5.6 convolution_convert_fusion.2
  621.2 2.7 convert_reduce_fusion.1
  623.9 10.3 %add_convert_fusion = bf16[768,2048]{1,0:T(8,128)(2,1)} fusion(bf16[768,2048]{1,0:T(8,128)(2,1)} %copy.17, bf16[768,2048]{0,1:T(8,128)(2,1)} %bitcast.101, f32[768,768]{1,0:T(8,128)} %convert_reduce_fusion.1), kind=kOutput, calls=%fused_computation.7 | convolution fusion | flops 3331129344 | bytes 11796480 | tf_op jit(solution)/shard_map/dot_general | solution.py:38
  634.2 5.5 convolution_convert_fusion.1
  639.7 2.7 convert_reduce_fusion
  642.4 8.7 %fusion.8 = bf16[1,768,2048]{2,1,0:T(8,128)(2,1)S(1)} fusion(bf16[768,2048]{1,0:T(8,128)(2,1)} %add_convert_fusion, f32[768,768]{1,0:T(8,128)} %convert_reduce_fusion), kind=kOutput, calls=%fused_computation.19 | convolution fusion | flops 3332702208 | bytes 8650752 | tf_op jit(solution)/shard_map/dot_general | solution.py:38
  651.2 0.1 fusion.41
  651.2 0.1 fusion.40
  651.3 0.1 fusion.39
  651.3 0.1 fusion.38
  651.4 0.1 fusion.37
  651.5 0.1 fusion.36
  651.5 0.1 fusion.35
  651.6 0.1 fusion.34
  651.7 0.0 copy-start.1
  651.7 72.9 %all_to_all.21 = bf16[8,1,768,256]{3,2,1,0:T(8,128)(2,1)S(1)} all-to-all(bf16[8,1,768,256]{3,2,1,0:T(8,128)(2,1)S(1)} %fusion.34), channel_id=1, replica_groups=mesh['dp'=8,'rep'=4] {'dp'}, dimensions={0} | all-to-all | bytes 6291456 | tf_op jit(solution)/shard_map/all_to_all | solution.py:107
  724.5 1.6 slice.46
  (8 shorter events, 0.0 us)
Async XLA Ops:
  6.5 123.4 %copy-start = (bf16[512,2048]{1,0:T(8,128)(2,1)S(1)}, bf16[512,2048]{1,0:T(8,128)(2,1)}, u32[]{:S(2)}) copy-start(bf16[512,2048]{1,0:T(8,128)(2,1)} %param.13) | copy-start | bytes 6291460
  6.5 105.1 %all-gather.2.cloned.1.call-start = ((), (), s32[]{:S(2)}) async-start(), calls=%async_computation.3 | async-start | bytes 7077888 | tf_op jit(solution)/shard_map/all_gather | solution.py:70
  7.3 448.8 %reduce-scatter.2.cloned.1.call-start = ((), (), s32[]{:S(2)}) async-start(), calls=%async_computation.4 | async-start | bytes 21233664 | tf_op jit(solution)/shard_map/reduce_scatter | solution.py:88
  124.5 5.5 copy-start.4
  147.4 365.9 %all-reduce.3.cloned.1.call-start = ((), (), s32[]{:S(2)}) async-start(), calls=%async_computation.5 | async-start | bytes 4718592 | tf_op jit(solution)/shard_map/psum | solution.py:91
  513.2 23.8 %copy-start.3 = (bf16[2,3,768,256]{3,2,1,0:T(8,128)(2,1)S(1)}, bf16[2,3,768,256]{3,2,1,0:T(8,128)(2,1)}, u32[]{:S(2)}) copy-start(bf16[2,3,768,256]{3,2,1,0:T(8,128)(2,1)} %all-reduce.3.cloned.1.call-done) | copy-start | bytes 7077892
  607.7 3.2 copy-start.2
  651.7 74.4 %copy-start.1 = (bf16[512,2048]{1,0:T(8,128)(2,1)S(1)}, bf16[512,2048]{1,0:T(8,128)(2,1)}, u32[]{:S(2)}) copy-start(bf16[512,2048]{1,0:T(8,128)(2,1)} %param.13) | copy-start | bytes 6291460
Sparse Core Ops, SparseCore 0:
  9.4 102.1 all-gather.1
  147.5 308.5 reduce-scatter.1
  458.4 54.7 all-reduce.2
